TPU v7x, 32 devices: a whole 2x2x4 slice. The times are simulated.
32 devices in a mesh: gx: 4 (over y, x), gy: 8 (over z, core).
Axes of the slice: x: 2, y: 2, z: 4, core: 2. Of those that a mesh axis runs over, the one named last changes fastest.
Arguments:
- tokens: bfloat16 [4096, 8192], P('gy', 'gx'), may hold values from -6 to 6
- pair_ids: int32 [8], replicated, may hold values from 0 to 7, each once
- query_weight: bfloat16 [8192, 8192], P('gy', 'gx'), may hold values from -0.0625 to 0.0625
- key_matrix: bfloat16 [8192, 1024], P('gy', 'gx'), may hold values from -0.0625 to 0.0625
- value_matrix: bfloat16 [8192, 1024], P('gy', 'gx'), may hold values from -0.0625 to 0.0625
- query_bias: bfloat16 [8192], P('gx'), may hold values from -13 to 13
- key_bias: bfloat16 [1024], P('gx'), may hold values from -8 to 8
- value_offset_bias: bfloat16 [1024], P('gx'), may hold values from -3 to 3
Outputs:
- attn_out: bfloat16 [4096, 8192], P('gy', 'gx')
Inputs may be any that keep to these rules, and one draw needn't show every extreme that they name: `pair_ids`: each number from 0 to 7 appears once.
All inputs are finite; a program needn't handle non-finite values.
Results may differ from a plain program's by a relative error of at most 0.0055.
The roundings to bfloat16 on the way count: a program that leaves them out, or rounds other values in their place, can miss the bound.
Values may be sent and summed in bfloat16 or wider, within the bound.
A program may use at most 128 MiB of HBM per device.

v0:
```python
import math
import jax
import jax.numpy as jnp
from jax import lax
from jax.sharding import PartitionSpec as P

HEAD_SIZE = 128
rope_theta = 1000000.0
neg_large = -1e30


def table_lookup(entries, wanted):
    slot_ids = lax.iota(jnp.int32, entries.shape[0])
    return jnp.sum(jnp.where(wanted[:, None] == slot_ids[None, :], entries[None, :], 0), axis=1)


def layout_positions(pair_ids, total_row_count, tok_dev):
    half_len = tok_dev // 2
    row_ids = lax.iota(jnp.int32, total_row_count)
    within = row_ids % tok_dev
    owners = table_lookup(pair_ids, row_ids // tok_dev)
    mirrored = 2 * pair_ids.shape[0] - 1 - owners
    return jnp.where(
        within < half_len, owners * half_len + within, mirrored * half_len + within - half_len
    )


def apply_rotary(values, token_positions):
    half_size = values.shape[-1] // 2
    frequency = jnp.exp(
        lax.iota(jnp.float32, half_size) * (-2.0 * math.log(rope_theta) / values.shape[-1])
    )
    angles = token_positions.astype(jnp.float32)[:, None] * frequency[None, :]
    cos_part = jnp.cos(angles)[:, None, :]
    sin_part = jnp.sin(angles)[:, None, :]
    lower_half = values[..., :half_size]
    upper_half = values[..., half_size:]
    return jnp.concatenate(
        [
            lower_half * cos_part - upper_half * sin_part,
            upper_half * cos_part + lower_half * sin_part,
        ],
        axis=-1,
    )


def absorb(running, query_block, key_block, value_block, visible):
    row_peak, totals, outputs = running
    scale = 1.0 / math.sqrt(query_block.shape[-1])
    scores = (
        jnp.einsum("hqd,khd->hqk", query_block, key_block, preferred_element_type=jnp.float32)
        * scale
    )
    if visible is not None:
        scores = jnp.where(visible[None], scores, neg_large)
    new_peak = jnp.maximum(row_peak, jnp.max(scores, axis=-1))
    weights = jnp.exp(scores - new_peak[..., None])
    if visible is not None:
        weights = jnp.where(visible[None], weights, 0.0)
    rescale = jnp.exp(row_peak - new_peak)
    totals = totals * rescale + jnp.sum(weights, axis=-1)
    outputs = outputs * rescale[..., None] + jnp.einsum(
        "hqk,khd->hqd",
        weights.astype(jnp.bfloat16),
        value_block,
        preferred_element_type=jnp.float32,
    )
    return (new_peak, totals, outputs)


def on_device(
    tokens,
    pair_ids,
    query_weight,
    key_matrix,
    value_matrix,
    query_bias,
    key_bias,
    value_offset_bias,
):
    tok_dev = tokens.shape[0]
    half_len = tok_dev // 2
    whole_rows = tok_dev * lax.axis_size("gy")
    kv_local = key_matrix.shape[1] // HEAD_SIZE
    q_local = query_weight.shape[1] // HEAD_SIZE
    query_group_width = q_local // kv_local
    gathered = lax.all_gather(tokens, "gx", axis=1, tiled=True)
    stacked = jnp.concatenate([query_weight, key_matrix, value_matrix], axis=1)
    projected = jnp.dot(
        gathered,
        lax.all_gather(stacked, "gy", axis=0, tiled=True),
        preferred_element_type=jnp.float32,
    )
    all_positions = layout_positions(pair_ids, whole_rows, tok_dev)
    own_index = lax.axis_index("gy")
    own_positions = lax.dynamic_slice_in_dim(all_positions, own_index * tok_dev, tok_dev, 0)
    own_pair = table_lookup(pair_ids, jnp.reshape(own_index, (1,)))[0]
    q_cols = q_local * HEAD_SIZE
    kv_cols = kv_local * HEAD_SIZE
    queries = projected[:, :q_cols] + query_bias.astype(jnp.float32)
    queries = apply_rotary(queries.reshape(tok_dev, q_local, HEAD_SIZE), own_positions).astype(
        jnp.bfloat16
    )
    projected_key_rows = projected[:, q_cols : q_cols + kv_cols] + key_bias.astype(jnp.float32)
    projected_key_rows = (
        apply_rotary(projected_key_rows.reshape(tok_dev, kv_local, HEAD_SIZE), own_positions)
        .astype(jnp.bfloat16)
        .reshape(tok_dev, kv_cols)
    )
    projected_value_rows = (
        projected[:, q_cols + kv_cols :] + value_offset_bias.astype(jnp.float32)
    ).astype(jnp.bfloat16)
    query_rows = (
        queries.reshape(tok_dev, kv_local, query_group_width, HEAD_SIZE)
        .transpose(1, 0, 2, 3)
        .reshape(kv_local, tok_dev * query_group_width, HEAD_SIZE)
    )
    row_positions = jnp.repeat(own_positions, query_group_width)
    row_total = tok_dev * query_group_width
    initial = (
        jnp.full((kv_local, row_total), neg_large, jnp.float32),
        jnp.zeros((kv_local, row_total), jnp.float32),
        jnp.zeros((kv_local, row_total, HEAD_SIZE), jnp.float32),
    )

    def paired(running, key_shard, value_shard, earlier):
        cut_rows = half_len * query_group_width
        former = tuple((member[:, :cut_rows] for member in running))
        latter = tuple((member[:, cut_rows:] for member in running))
        query_former = query_rows[:, :cut_rows]
        query_latter = query_rows[:, cut_rows:]
        latter = absorb(latter, query_latter, key_shard[:half_len], value_shard[:half_len], None)
        picked_state = tuple(
            (jnp.where(earlier, left, right) for left, right in zip(former, latter))
        )
        query_pick = jnp.where(earlier, query_former, query_latter)
        key_pick = jnp.where(earlier, key_shard[:half_len], key_shard[half_len:])
        value_pick = jnp.where(earlier, value_shard[:half_len], value_shard[half_len:])
        updated = absorb(picked_state, query_pick, key_pick, value_pick, None)
        former = tuple((jnp.where(earlier, fresh, kept) for fresh, kept in zip(updated, former)))
        latter = tuple((jnp.where(earlier, kept, fresh) for fresh, kept in zip(updated, latter)))
        return tuple(
            (jnp.concatenate([left, right], axis=1) for left, right in zip(former, latter))
        )

    key_piece = lax.all_gather(projected_key_rows, "gy", axis=0, tiled=True)
    value_piece = lax.all_gather(projected_value_rows, "gy", axis=0, tiled=True)
    total_row_count = key_piece.shape[0]

    def one_shard(shard_index, carried):
        begin = shard_index * tok_dev
        key_shard = lax.dynamic_slice_in_dim(key_piece, begin, tok_dev, 0).reshape(
            tok_dev, kv_local, HEAD_SIZE
        )
        value_shard = lax.dynamic_slice_in_dim(value_piece, begin, tok_dev, 0).reshape(
            tok_dev, kv_local, HEAD_SIZE
        )
        source = jnp.reshape(begin // tok_dev, (1,))
        their_pair = table_lookup(pair_ids, source)[0]

        def itself(state_in):
            key_positions = lax.dynamic_slice_in_dim(all_positions, begin, tok_dev, 0)
            visible = key_positions[None, :] <= row_positions[:, None]
            return absorb(state_in, query_rows, key_shard, value_shard, visible)

        def elsewhere(state_in):
            return paired(state_in, key_shard, value_shard, their_pair < own_pair)

        return lax.cond(their_pair == own_pair, itself, elsewhere, carried)

    row_peak, totals, outputs = lax.fori_loop(0, total_row_count // tok_dev, one_shard, initial)
    normalized = (outputs / totals[..., None]).astype(jnp.bfloat16)
    return (
        normalized.reshape(kv_local, tok_dev, query_group_width, HEAD_SIZE)
        .transpose(1, 0, 2, 3)
        .reshape(tok_dev, q_cols)
    )


def solution(mesh):
    in_specs = (
        P("gy", "gx"),
        P(),
        P("gy", "gx"),
        P("gy", "gx"),
        P("gy", "gx"),
        P("gx"),
        P("gx"),
        P("gx"),
    )
    out_specs = P("gy", "gx")
    return jax.shard_map(
        on_device, mesh=mesh, in_specs=in_specs, out_specs=out_specs, check_vma=False
    )
```

profile of v0, /device:TPU:0, one launch (start us, length us, event | category | flops | bytes accessed | tf_op | source)
XLA Modules:
  0.0 768.3 jit_solution(7641844237663635094)
XLA Ops:
  7.3 6.9 pad_maximum_fusion.3
  15.7 83.8 %all-gather.7.cloned.1.call-done = bf16[512,8192]{1,0:T(8,128)(2,1)} async-done(((bf16[512,2048]{1,0:T(8,128)(2,1)}), bf16[512,8192]{1,0:T(8,128)(2,1)}) %all-gather.7.cloned.1.call-update) | async-done | bytes 8388624 | tf_op jit(solution)/shard_map/all_gather | solution.py:87
  99.4 360.5 %all-gather.5.cloned.1.call-done = bf16[8192,2560]{1,0:T(8,128)(2,1)} async-done(((bf16[1024,2560]{1,0:T(8,128)(2,1)}), bf16[8192,2560]{1,0:T(8,128)(2,1)}) %all-gather.5.cloned.1.call-update) | async-done | bytes 41943056 | tf_op jit(solution)/shard_map/all_gather | solution.py:91
  459.9 30.0 %convolution_bitcast_fusion = f32[512,2560]{0,1:T(8,128)} fusion(bf16[8192,2560]{1,0:T(8,128)(2,1)} %all-gather.5.cloned.1.call-done, bf16[512,8192]{1,0:T(8,128)(2,1)} %all-gather.7.cloned.1.call-done), kind=kOutput, calls=%fused_computation.67 | convolution fusion | flops 21474836480 | bytes 55574528 | tf_op jit(solution)/shard_map/dot_general | solution.py:89
  503.4 4.1 maximum_bitcast_fusion
  507.5 13.1 %all-gather.9.cloned.1.call-done = bf16[4096,256]{0,1:T(8,128)(2,1)} async-done(((bf16[512,256]{0,1:T(8,128)(2,1)}), bf16[4096,256]{0,1:T(8,128)(2,1)}) %all-gather.9.cloned.1.call-update) | async-done | bytes 2097168 | tf_op jit(solution)/shard_map/all_gather | solution.py:146
  520.6 30.0 %all-gather.11.cloned.1.call-done = bf16[4096,256]{0,1:T(8,128)(2,1)} async-done(((bf16[512,256]{0,1:T(8,128)(2,1)}), bf16[4096,256]{0,1:T(8,128)(2,1)}) %all-gather.11.cloned.1.call-update) | async-done | bytes 2097168 | tf_op jit(solution)/shard_map/all_gather | solution.py:147
  553.5 203.1 %while.20 = (s32[]{:T(128)}, f32[2,4096]{1,0:T(2,128)S(1)}, f32[2,4096]{1,0:T(2,128)}, f32[2,4096,128]{2,1,0:T(8,128)}, s32[8]{0:T(128)S(1)}, /*index=5*/s32[]{:...) while((s32[]{:T(128)}, f32[2,4096]{1,0:T(2,128)S(1)}, ...), condition=%wide.region_12.13_spmd.clone, body=%wide.region_2.12_spmd.clone.sunk | while | flops 2206220288 | bytes 138748624 | solution.py:171
  556.6 28.6 %conditional.3 = (f32[2,4096]{1,0:T(2,128)}, f32[2,4096]{1,0:T(2,128)}, f32[2,4096,128]{2,1,0:T(8,128)}) conditional(s32[]{:T(128)} %convert_element_type.69, (s32[]{:T(128)}, s32[]{:T(128)}, f32[2,4096]{1,0:T(2,128)S(1)}, bf16[2,4096,128]{2,1,0:T(8,128)(2,1)}, bf16[512,2,128]{0,2,1:T(8,128)(2,1)S(1)}, /*index=5*/f32[2,4096]{1,0:T(2,128)}, ...), branch_computations={%region_4.8_spmd, %region_9.11_spmd} | conditional | flops 2206220288 | bytes 137633952 | solution.py:169
  558.3 5.8 fusion.28
  566.1 5.3 fusion.30
  572.9 12.3 %fusion.34 = f32[2,4096,128]{2,1,0:T(8,128)} fusion(bf16[512,2,128]{0,2,1:T(8,128)(2,1)S(1)} %get-tuple-element.414, f32[2,4096,512]{1,2,0:T(8,128)} %copy-done.3, f32[2,4096]{1,0:T(2,128)} %max.8, pred[4096,512]{0,1:T(8,128)(4,1)S(1)} %broadcast_compare_fusion, f32[2,4096,128]{2,1,0:T(8,128)} %get-tuple-element.321, f32[2,4096]{1,0:T(2,128)S(1)} %get-tuple-element.446), kind=kOutput, calls=%fused_computation.55 | convolution fusion | flops 1096810496 | bytes 27590656 | tf_op jit(solution)/shard_map/while/body/eval_jaxpr/cond/branch_1_fun/hqk,khd->hqd/dot_general | solution.py:62
  589.0 20.6 %conditional.3 = (f32[2,4096]{1,0:T(2,128)}, f32[2,4096]{1,0:T(2,128)}, f32[2,4096,128]{2,1,0:T(8,128)}) conditional(s32[]{:T(128)} %convert_element_type.69, (s32[]{:T(128)}, s32[]{:T(128)}, f32[2,4096]{1,0:T(2,128)S(1)}, bf16[2,4096,128]{2,1,0:T(8,128)(2,1)}, bf16[512,2,128]{0,2,1:T(8,128)(2,1)S(1)}, /*index=5*/f32[2,4096]{1,0:T(2,128)}, ...), branch_computations={%region_4.8_spmd, %region_9.11_spmd} | conditional | flops 2206220288 | bytes 137633952 | solution.py:169
  598.4 4.4 convolution_add_fusion.1
  613.4 20.6 %conditional.3 = (f32[2,4096]{1,0:T(2,128)}, f32[2,4096]{1,0:T(2,128)}, f32[2,4096,128]{2,1,0:T(8,128)}) conditional(s32[]{:T(128)} %convert_element_type.69, (s32[]{:T(128)}, s32[]{:T(128)}, f32[2,4096]{1,0:T(2,128)S(1)}, bf16[2,4096,128]{2,1,0:T(8,128)(2,1)}, bf16[512,2,128]{0,2,1:T(8,128)(2,1)S(1)}, /*index=5*/f32[2,4096]{1,0:T(2,128)}, ...), branch_computations={%region_4.8_spmd, %region_9.11_spmd} | conditional | flops 2206220288 | bytes 137633952 | solution.py:169
  617.1 2.8 multiply_reduce_fusion.1
  622.8 4.4 convolution_add_fusion.1
  637.8 20.6 %conditional.3 = (f32[2,4096]{1,0:T(2,128)}, f32[2,4096]{1,0:T(2,128)}, f32[2,4096,128]{2,1,0:T(8,128)}) conditional(s32[]{:T(128)} %convert_element_type.69, (s32[]{:T(128)}, s32[]{:T(128)}, f32[2,4096]{1,0:T(2,128)S(1)}, bf16[2,4096,128]{2,1,0:T(8,128)(2,1)}, bf16[512,2,128]{0,2,1:T(8,128)(2,1)S(1)}, /*index=5*/f32[2,4096]{1,0:T(2,128)}, ...), branch_computations={%region_4.8_spmd, %region_9.11_spmd} | conditional | flops 2206220288 | bytes 137633952 | solution.py:169
  641.5 2.8 multiply_reduce_fusion.1
  647.2 4.4 convolution_add_fusion.1
  662.2 20.6 %conditional.3 = (f32[2,4096]{1,0:T(2,128)}, f32[2,4096]{1,0:T(2,128)}, f32[2,4096,128]{2,1,0:T(8,128)}) conditional(s32[]{:T(128)} %convert_element_type.69, (s32[]{:T(128)}, s32[]{:T(128)}, f32[2,4096]{1,0:T(2,128)S(1)}, bf16[2,4096,128]{2,1,0:T(8,128)(2,1)}, bf16[512,2,128]{0,2,1:T(8,128)(2,1)S(1)}, /*index=5*/f32[2,4096]{1,0:T(2,128)}, ...), branch_computations={%region_4.8_spmd, %region_9.11_spmd} | conditional | flops 2206220288 | bytes 137633952 | solution.py:169
  665.9 2.8 multiply_reduce_fusion.1
  671.6 4.4 convolution_add_fusion.1
  686.6 20.6 %conditional.3 = (f32[2,4096]{1,0:T(2,128)}, f32[2,4096]{1,0:T(2,128)}, f32[2,4096,128]{2,1,0:T(8,128)}) conditional(s32[]{:T(128)} %convert_element_type.69, (s32[]{:T(128)}, s32[]{:T(128)}, f32[2,4096]{1,0:T(2,128)S(1)}, bf16[2,4096,128]{2,1,0:T(8,128)(2,1)}, bf16[512,2,128]{0,2,1:T(8,128)(2,1)S(1)}, /*index=5*/f32[2,4096]{1,0:T(2,128)}, ...), branch_computations={%region_4.8_spmd, %region_9.11_spmd} | conditional | flops 2206220288 | bytes 137633952 | solution.py:169
  690.3 2.8 multiply_reduce_fusion.1
  696.0 4.4 convolution_add_fusion.1
  710.9 20.6 %conditional.3 = (f32[2,4096]{1,0:T(2,128)}, f32[2,4096]{1,0:T(2,128)}, f32[2,4096,128]{2,1,0:T(8,128)}) conditional(s32[]{:T(128)} %convert_element_type.69, (s32[]{:T(128)}, s32[]{:T(128)}, f32[2,4096]{1,0:T(2,128)S(1)}, bf16[2,4096,128]{2,1,0:T(8,128)(2,1)}, bf16[512,2,128]{0,2,1:T(8,128)(2,1)S(1)}, /*index=5*/f32[2,4096]{1,0:T(2,128)}, ...), branch_computations={%region_4.8_spmd, %region_9.11_spmd} | conditional | flops 2206220288 | bytes 137633952 | solution.py:169
  720.4 4.4 convolution_add_fusion.1
  735.3 20.6 %conditional.3 = (f32[2,4096]{1,0:T(2,128)}, f32[2,4096]{1,0:T(2,128)}, f32[2,4096,128]{2,1,0:T(8,128)}) conditional(s32[]{:T(128)} %convert_element_type.69, (s32[]{:T(128)}, s32[]{:T(128)}, f32[2,4096]{1,0:T(2,128)S(1)}, bf16[2,4096,128]{2,1,0:T(8,128)(2,1)}, bf16[512,2,128]{0,2,1:T(8,128)(2,1)S(1)}, /*index=5*/f32[2,4096]{1,0:T(2,128)}, ...), branch_computations={%region_4.8_spmd, %region_9.11_spmd} | conditional | flops 2206220288 | bytes 137633952 | solution.py:169
  739.1 2.8 multiply_reduce_fusion.1
  744.8 4.4 convolution_add_fusion.1
  756.7 2.9 fusion.41
  (209 shorter events, 136.1 us)
Async XLA Ops:
  6.5 92.9 %all-gather.7.cloned.1.call-start = ((), (), s32[]{:S(2)}) async-start(), calls=%async_computation.1 | async-start | bytes 10485760 | tf_op jit(solution)/shard_map/all_gather | solution.py:87
  7.3 452.7 %all-gather.5.cloned.1.call-start = ((), (), s32[]{:S(2)}) async-start(), calls=%async_computation | async-start | bytes 47185920 | tf_op jit(solution)/shard_map/all_gather | solution.py:91
  14.2 506.4 %all-gather.9.cloned.1.call-start = ((), (), s32[]{:S(2)}) async-start(), calls=%async_computation.2 | async-start | bytes 2359296 | tf_op jit(solution)/shard_map/all_gather | solution.py:146
  15.6 477.7 %copy-start.7 = (bf16[2048]{0:T(1024)(128)(2,1)S(1)}, bf16[2048]{0:T(1024)(128)(2,1)}, u32[]{:S(2)}) copy-start(bf16[2048]{0:T(1024)(128)(2,1)} %param.17) | copy-start | bytes 12292
  492.8 57.9 %all-gather.11.cloned.1.call-start = ((), (), s32[]{:S(2)}) async-start(), calls=%async_computation.3 | async-start | bytes 2359296 | tf_op jit(solution)/shard_map/all_gather | solution.py:147
  564.2 7.2 copy-start.3
  566.1 5.3 copy-start.6
  592.7 4.3 copy-start
  595.5 2.0 copy-start.2
  598.4 4.4 copy-start.1
  598.4 5.3 copy-start.4
  617.1 4.3 copy-start
  619.9 2.0 copy-start.2
  622.8 4.4 copy-start.1
  622.8 5.3 copy-start.4
  641.5 4.3 copy-start
  644.3 2.0 copy-start.2
  647.2 4.4 copy-start.1
  647.2 5.3 copy-start.4
  665.9 4.3 copy-start
  668.6 2.0 copy-start.2
  671.6 4.4 copy-start.1
  671.6 5.3 copy-start.4
  690.3 4.3 copy-start
  696.0 4.4 copy-start.1
  696.0 5.3 copy-start.4
  714.7 4.3 copy-start
  720.4 4.4 copy-start.1
  720.4 5.3 copy-start.4
  739.0 4.3 copy-start
  744.8 4.4 copy-start.1
  744.8 5.3 copy-start.4
  (7 other events, 9.6 us)
Sparse Core Ops, SparseCore 0:
  9.2 90.1 all-gather.6
  101.1 358.8 all-gather.4
  492.9 27.7 all-gather.8
  522.1 28.5 all-gather.10
where the time goes:
time: 771 us; the launch traced here: 768 us
  waiting for transfers between devices  489 us (63%)
  matrix products  126 us (16%)
  other arithmetic  83.3 us (11%)
  local copies, waits for them, and re-layouts  37.8 us (5%)
  loops' own time  19.6 us (3%)
  between operations  13.2 us (2%)
    all_gather x1, waiting for transfers between devices, on_device(): lax.all_gather(stacked, 'gy', axis=0, tiled=True)  361 us
    all_gather x1, waiting for transfers between devices, on_device(): gathered = lax.all_gather(tokens, 'gx', axis=1, tiled=True)  83.8 us
    dot_general x15, matrix products, absorb(): jnp.einsum('hqk,khd->hqd', weights.astype(jnp.bfloat16), value_block, pre...  54.5 us
    dot_general x15, matrix products, absorb(): jnp.einsum('hqd,khd->hqk', query_block, key_block, preferred_element_type...  41.1 us
    all_gather x1, waiting for transfers between devices, on_device(): value_piece = lax.all_gather(projected_value_rows, 'gy', axis=0, tiled=True)  30 us
    dot_general x1, matrix products, on_device(): jnp.dot(gathered, lax.all_gather(stacked, 'gy', axis=0, tiled=True), pref...  30 us
    concatenate x21, other arithmetic, paired(): jnp.concatenate([left, right], axis=1)  24.3 us
    reduce_sum x8, other arithmetic, absorb(): totals = totals * rescale + jnp.sum(weights, axis=-1)  15.5 us
  transfers between devices with their start and end apart: 4, of which 4 were waited for; matrix products, arithmetic and copies ran while one was open for 3% of the time, Pallas kernels for 0%

commit v1 on v0

--- a/solution.py
+++ b/solution.py
@@ -7,6 +7,22 @@
 HEAD_SIZE = 128
 rope_theta = 1000000.0
 neg_large = -1e30
+
+
+def change_side(x_in):
+    history = []
+    chips = lax.axis_size("gx")
+    for no in range(1, chips):
+        history.append((no - 1, no))
+    b_next = history + [(chips - 1, 0)]
+    now = x_in
+    xs_all = [now]
+    for _ in range(chips - 1):
+        now = lax.ppermute(now, "gx", b_next)
+        xs_all += [now]
+    big = jnp.concatenate([*reversed(xs_all)], axis=1)
+    current_block = jnp.roll(big, (lax.axis_index("gx") + 1) * now.shape[1], axis=1)
+    return current_block
 
 
 def table_lookup(entries, wanted):
@@ -84,7 +100,7 @@
     kv_local = key_matrix.shape[1] // HEAD_SIZE
     q_local = query_weight.shape[1] // HEAD_SIZE
     query_group_width = q_local // kv_local
-    gathered = lax.all_gather(tokens, "gx", axis=1, tiled=True)
+    gathered = change_side(tokens)
     stacked = jnp.concatenate([query_weight, key_matrix, value_matrix], axis=1)
     projected = jnp.dot(
         gathered,

time: 771 us -> 696 us (0.903)
  waiting for transfers between devices: 489 us -> 385 us
  local copies, waits for them, and re-layouts: 37.8 us -> 65.6 us
    all_gather x1, waiting for transfers between devices: 361 us -> 196 us  [on_device(): lax.all_gather(stacked, 'gy', axis=0, tiled=True)]
    ppermute x0 -> x3, waiting for transfers between devices: none -> 140 us  [change_side(): now = lax.ppermute(now, 'gx', b_next)]
    all_gather x1 -> x0, waiting for transfers between devices: 83.8 us -> none  [on_device(): gathered = lax.all_gather(tokens, 'gx', axis=1, tiled=True)]
    unnamed x9 -> x25, local copies, waits for them, and re-layouts: 2.45 us -> 24.7 us
    dynamic_slice x0 -> x8, local copies, waits for them, and re-layouts: none -> 7.8 us  [one_shard(): lax.dynamic_slice_in_dim(key_piece, begin, tok_dev, 0)]
  transfers between devices with their start and end apart: 4 -> 6, of which waited for: 4 -> 6; matrix products, arithmetic and copies ran while one was open for 3% -> 4% of each run, Pallas kernels for 0% -> 0%
where the time goes in v1:
time: 696 us; the launch traced here: 693 us
  waiting for transfers between devices  385 us (55%)
  matrix products  123 us (18%)
  other arithmetic  81.1 us (12%)
  local copies, waits for them, and re-layouts  65.6 us (9%)
  loops' own time  20.8 us (3%)
  between operations  13.3 us (2%)
    all_gather x1, waiting for transfers between devices, on_device(): lax.all_gather(stacked, 'gy', axis=0, tiled=True)  196 us
    ppermute x3, waiting for transfers between devices, change_side(): now = lax.ppermute(now, 'gx', b_next)  140 us
    dot_general x15, matrix products, absorb(): jnp.einsum('hqk,khd->hqd', weights.astype(jnp.bfloat16), value_block, pre...  54.5 us
    dot_general x15, matrix products, absorb(): jnp.einsum('hqd,khd->hqk', query_block, key_block, preferred_element_type...  41.1 us
    all_gather x1, waiting for transfers between devices, on_device(): value_piece = lax.all_gather(projected_value_rows, 'gy', axis=0, tiled=True)  30.2 us
    dot_general x1, matrix products, on_device(): jnp.dot(gathered, lax.all_gather(stacked, 'gy', axis=0, tiled=True), pref...  27 us
    unnamed x25, local copies, waits for them, and re-layouts  24.7 us
    concatenate x21, other arithmetic, paired(): jnp.concatenate([left, right], axis=1)  24.2 us
  transfers between devices with their start and end apart: 6, of which 6 were waited for; matrix products, arithmetic and copies ran while one was open for 4% of the time, Pallas kernels for 0%

profile of v1, /device:TPU:0, one launch (start us, length us, event | category | flops | bytes accessed | tf_op | source)
XLA Modules:
  0.0 692.6 jit_solution(106286395317263812)
XLA Ops:
  6.5 6.9 pad_maximum_fusion.3
  15.0 3.0 collective-permute-start
  18.0 46.6 %collective-permute-done = bf16[512,2048]{1,0:T(8,128)(2,1)S(1)} collective-permute-done((bf16[512,2048]{1,0:T(8,128)(2,1)S(1)}, bf16[512,2048]{1,0:T(8,128)(2,1)S(1)}, u32[]{:S(2)}, u32[]{:S(2)}) %collective-permute-start) | collective-permute-done | bytes 2097184 | tf_op jit(solution)/shard_map/ppermute | solution.py:21
  66.7 47.1 %collective-permute-done.1 = bf16[512,2048]{1,0:T(8,128)(2,1)} collective-permute-done((bf16[512,2048]{1,0:T(8,128)(2,1)S(1)}, bf16[512,2048]{1,0:T(8,128)(2,1)}, u32[]{:S(2)}, u32[]{:S(2)}) %collective-permute-start.1) | collective-permute-done | bytes 2097184 | tf_op jit(solution)/shard_map/ppermute | solution.py:21
  115.1 46.0 %collective-permute-done.2 = bf16[512,2048]{1,0:T(8,128)(2,1)} collective-permute-done((bf16[512,2048]{1,0:T(8,128)(2,1)}, bf16[512,2048]{1,0:T(8,128)(2,1)}, u32[]{:S(2)}, u32[]{:S(2)}) %collective-permute-start.2) | collective-permute-done | bytes 2097184 | tf_op jit(solution)/shard_map/ppermute | solution.py:21
  161.1 3.2 constant_dynamic-update-slice_fusion.7
  164.3 3.1 constant_dynamic-update-slice_fusion.6
  170.2 3.1 constant_dynamic-update-slice_fusion.3
  173.3 3.1 constant_dynamic-update-slice_fusion.2
  179.3 195.9 %all-gather.4.cloned.1.call-done = bf16[8192,2560]{1,0:T(8,128)(2,1)} async-done(((bf16[1024,2560]{1,0:T(8,128)(2,1)}), bf16[8192,2560]{1,0:T(8,128)(2,1)}) %all-gather.4.cloned.1.call-update) | async-done | bytes 41943056 | tf_op jit(solution)/shard_map/all_gather | solution.py:107
  375.2 27.0 %fusion.41 = f32[512,2560]{1,0:T(8,128)S(1)} fusion(bf16[8192,2560]{1,0:T(8,128)(2,1)} %all-gather.4.cloned.1.call-done, bf16[512,16384]{1,0:T(8,128)(2,1)} %constant_dynamic-update-slice_fusion, s32[]{:T(128)S(6)} %select_n.157), kind=kOutput, calls=%fused_computation.66 | convolution fusion | flops 21474836480 | bytes 55574532 | tf_op jit(solution)/shard_map/dot_general | solution.py:105
  417.1 18.8 %all-gather.6.cloned.1.call-done = bf16[4096,256]{0,1:T(8,128)(2,1)} async-done(((bf16[512,256]{0,1:T(8,128)(2,1)}), bf16[4096,256]{0,1:T(8,128)(2,1)}) %all-gather.6.cloned.1.call-update) | async-done | bytes 2097168 | tf_op jit(solution)/shard_map/all_gather | solution.py:162
  435.9 30.2 %all-gather.8.cloned.1.call-done = bf16[4096,256]{1,0:T(8,128)(2,1)} async-done(((bf16[512,256]{1,0:T(8,128)(2,1)}), bf16[4096,256]{1,0:T(8,128)(2,1)}) %all-gather.8.cloned.1.call-update) | async-done | bytes 2097168 | tf_op jit(solution)/shard_map/all_gather | solution.py:163
  468.9 212.0 %while.20 = (s32[]{:T(128)}, f32[2,4096]{1,0:T(2,128)S(1)}, f32[2,4096]{1,0:T(2,128)}, f32[2,4096,128]{2,1,0:T(8,128)}, s32[8]{0:T(128)S(1)}, /*index=5*/s32[]{:...) while((s32[]{:T(128)}, f32[2,4096]{1,0:T(2,128)S(1)}, ...), condition=%wide.region_12.13_spmd.clone, body=%wide.region_2.12_spmd.clone.sunk | while | flops 2206220288 | bytes 139272912 | solution.py:187
  473.0 28.6 %conditional.3 = (f32[2,4096]{1,0:T(2,128)}, f32[2,4096]{1,0:T(2,128)}, f32[2,4096,128]{2,1,0:T(8,128)}) conditional(s32[]{:T(128)} %convert_element_type.69, (s32[]{:T(128)}, s32[]{:T(128)}, f32[2,4096]{1,0:T(2,128)S(1)}, bf16[2,4096,128]{2,1,0:T(8,128)(2,1)}, bf16[512,2,128]{0,2,1:T(8,128)(2,1)S(1)}, /*index=5*/f32[2,4096]{1,0:T(2,128)}, ...), branch_computations={%region_4.8_spmd, %region_9.11_spmd} | conditional | flops 2206220288 | bytes 137633952 | solution.py:185
  474.7 5.8 fusion.28
  482.5 5.3 fusion.30
  489.3 12.4 %fusion.34 = f32[2,4096,128]{2,1,0:T(8,128)} fusion(bf16[512,2,128]{0,2,1:T(8,128)(2,1)S(1)} %get-tuple-element.414, f32[2,4096,512]{1,2,0:T(8,128)} %copy-done.3, f32[2,4096]{1,0:T(2,128)} %max.8, pred[4096,512]{0,1:T(8,128)(4,1)S(1)} %broadcast_compare_fusion, f32[2,4096,128]{2,1,0:T(8,128)} %get-tuple-element.321, f32[2,4096]{1,0:T(2,128)S(1)} %get-tuple-element.457), kind=kOutput, calls=%fused_computation.55 | convolution fusion | flops 1096810496 | bytes 27590656 | tf_op jit(solution)/shard_map/while/body/eval_jaxpr/cond/branch_1_fun/hqk,khd->hqd/dot_general | solution.py:78
  506.5 20.7 %conditional.3 = (f32[2,4096]{1,0:T(2,128)}, f32[2,4096]{1,0:T(2,128)}, f32[2,4096,128]{2,1,0:T(8,128)}) conditional(s32[]{:T(128)} %convert_element_type.69, (s32[]{:T(128)}, s32[]{:T(128)}, f32[2,4096]{1,0:T(2,128)S(1)}, bf16[2,4096,128]{2,1,0:T(8,128)(2,1)}, bf16[512,2,128]{0,2,1:T(8,128)(2,1)S(1)}, /*index=5*/f32[2,4096]{1,0:T(2,128)}, ...), branch_computations={%region_4.8_spmd, %region_9.11_spmd} | conditional | flops 2206220288 | bytes 137633952 | solution.py:185
  516.0 4.4 convolution_add_fusion.1
  532.0 20.7 %conditional.3 = (f32[2,4096]{1,0:T(2,128)}, f32[2,4096]{1,0:T(2,128)}, f32[2,4096,128]{2,1,0:T(8,128)}) conditional(s32[]{:T(128)} %convert_element_type.69, (s32[]{:T(128)}, s32[]{:T(128)}, f32[2,4096]{1,0:T(2,128)S(1)}, bf16[2,4096,128]{2,1,0:T(8,128)(2,1)}, bf16[512,2,128]{0,2,1:T(8,128)(2,1)S(1)}, /*index=5*/f32[2,4096]{1,0:T(2,128)}, ...), branch_computations={%region_4.8_spmd, %region_9.11_spmd} | conditional | flops 2206220288 | bytes 137633952 | solution.py:185
  541.5 4.4 convolution_add_fusion.1
  557.5 20.7 %conditional.3 = (f32[2,4096]{1,0:T(2,128)}, f32[2,4096]{1,0:T(2,128)}, f32[2,4096,128]{2,1,0:T(8,128)}) conditional(s32[]{:T(128)} %convert_element_type.69, (s32[]{:T(128)}, s32[]{:T(128)}, f32[2,4096]{1,0:T(2,128)S(1)}, bf16[2,4096,128]{2,1,0:T(8,128)(2,1)}, bf16[512,2,128]{0,2,1:T(8,128)(2,1)S(1)}, /*index=5*/f32[2,4096]{1,0:T(2,128)}, ...), branch_computations={%region_4.8_spmd, %region_9.11_spmd} | conditional | flops 2206220288 | bytes 137633952 | solution.py:185
  567.0 4.4 convolution_add_fusion.1
  583.0 20.7 %conditional.3 = (f32[2,4096]{1,0:T(2,128)}, f32[2,4096]{1,0:T(2,128)}, f32[2,4096,128]{2,1,0:T(8,128)}) conditional(s32[]{:T(128)} %convert_element_type.69, (s32[]{:T(128)}, s32[]{:T(128)}, f32[2,4096]{1,0:T(2,128)S(1)}, bf16[2,4096,128]{2,1,0:T(8,128)(2,1)}, bf16[512,2,128]{0,2,1:T(8,128)(2,1)S(1)}, /*index=5*/f32[2,4096]{1,0:T(2,128)}, ...), branch_computations={%region_4.8_spmd, %region_9.11_spmd} | conditional | flops 2206220288 | bytes 137633952 | solution.py:185
  592.5 4.4 convolution_add_fusion.1
  608.5 20.7 %conditional.3 = (f32[2,4096]{1,0:T(2,128)}, f32[2,4096]{1,0:T(2,128)}, f32[2,4096,128]{2,1,0:T(8,128)}) conditional(s32[]{:T(128)} %convert_element_type.69, (s32[]{:T(128)}, s32[]{:T(128)}, f32[2,4096]{1,0:T(2,128)S(1)}, bf16[2,4096,128]{2,1,0:T(8,128)(2,1)}, bf16[512,2,128]{0,2,1:T(8,128)(2,1)S(1)}, /*index=5*/f32[2,4096]{1,0:T(2,128)}, ...), branch_computations={%region_4.8_spmd, %region_9.11_spmd} | conditional | flops 2206220288 | bytes 137633952 | solution.py:185
  618.0 4.4 convolution_add_fusion.1
  634.0 20.7 %conditional.3 = (f32[2,4096]{1,0:T(2,128)}, f32[2,4096]{1,0:T(2,128)}, f32[2,4096,128]{2,1,0:T(8,128)}) conditional(s32[]{:T(128)} %convert_element_type.69, (s32[]{:T(128)}, s32[]{:T(128)}, f32[2,4096]{1,0:T(2,128)S(1)}, bf16[2,4096,128]{2,1,0:T(8,128)(2,1)}, bf16[512,2,128]{0,2,1:T(8,128)(2,1)S(1)}, /*index=5*/f32[2,4096]{1,0:T(2,128)}, ...), branch_computations={%region_4.8_spmd, %region_9.11_spmd} | conditional | flops 2206220288 | bytes 137633952 | solution.py:185
  643.5 4.4 convolution_add_fusion.1
  659.5 20.7 %conditional.3 = (f32[2,4096]{1,0:T(2,128)}, f32[2,4096]{1,0:T(2,128)}, f32[2,4096,128]{2,1,0:T(8,128)}) conditional(s32[]{:T(128)} %convert_element_type.69, (s32[]{:T(128)}, s32[]{:T(128)}, f32[2,4096]{1,0:T(2,128)S(1)}, bf16[2,4096,128]{2,1,0:T(8,128)(2,1)}, bf16[512,2,128]{0,2,1:T(8,128)(2,1)S(1)}, /*index=5*/f32[2,4096]{1,0:T(2,128)}, ...), branch_computations={%region_4.8_spmd, %region_9.11_spmd} | conditional | flops 2206220288 | bytes 137633952 | solution.py:185
  669.0 4.4 convolution_add_fusion.1
  (245 shorter events, 170.2 us)
Async XLA Ops:
  6.5 368.7 %all-gather.4.cloned.1.call-start = ((), (), s32[]{:S(2)}) async-start(), calls=%async_computation | async-start | bytes 47185920 | tf_op jit(solution)/shard_map/all_gather | solution.py:107
  13.4 100.4 %copy-start.13 = (bf16[256]{0:T(256)(128)(2,1)S(1)}, bf16[256]{0:T(256)(128)(2,1)}, u32[]{:S(2)}) copy-start(bf16[256]{0:T(256)(128)(2,1)} %param.18) | copy-start | bytes 1540
  13.4 100.4 %copy-start.14 = (bf16[256]{0:T(256)(128)(2,1)S(1)}, bf16[256]{0:T(256)(128)(2,1)}, u32[]{:S(2)}) copy-start(bf16[256]{0:T(256)(128)(2,1)} %param.19) | copy-start | bytes 1540
  13.4 100.4 %copy-start.12 = (s32[8]{0:T(128)S(1)}, s32[8]{0:T(128)}, u32[]{:S(2)}) copy-start(s32[8]{0:T(128)} %param.13) | copy-start | bytes 100
  13.5 422.4 %all-gather.6.cloned.1.call-start = ((), (), s32[]{:S(2)}) async-start(), calls=%async_computation.1 | async-start | bytes 2359296 | tf_op jit(solution)/shard_map/all_gather | solution.py:162
  15.0 49.5 %collective-permute-start = (bf16[512,2048]{1,0:T(8,128)(2,1)S(1)}, bf16[512,2048]{1,0:T(8,128)(2,1)S(1)}, u32[]{:S(2)}, u32[]{:S(2)}) collective-permute-start(bf16[512,2048]{1,0:T(8,128)(2,1)S(1)} %copy-done.7), channel_id=1, source_target_pairs={{0,8},{8,16},{16,24},{24,0},{1,9},{9,17},{17,25},{25,1},{2,10},{10... | collective-permute-start | bytes 6291464 | tf_op jit(solution)/shard_map/ppermute | solution.py:21
  65.9 47.9 %collective-permute-start.1 = (bf16[512,2048]{1,0:T(8,128)(2,1)S(1)}, bf16[512,2048]{1,0:T(8,128)(2,1)}, u32[]{:S(2)}, u32[]{:S(2)}) collective-permute-start(bf16[512,2048]{1,0:T(8,128)(2,1)S(1)} %collective-permute-done), channel_id=1, source_target_pairs={{0,8},{8,16},{16,24},{24,0},{1,9},{9,17},{17,25},{25,1},{2,10},{10... | collective-permute-start | bytes 6291464 | tf_op jit(solution)/shard_map/ppermute | solution.py:21
  113.8 47.3 %collective-permute-start.2 = (bf16[512,2048]{1,0:T(8,128)(2,1)}, bf16[512,2048]{1,0:T(8,128)(2,1)}, u32[]{:S(2)}, u32[]{:S(2)}) collective-permute-start(bf16[512,2048]{1,0:T(8,128)(2,1)} %collective-permute-done.1), channel_id=1, source_target_pairs={{0,8},{8,16},{16,24},{24,0},{1,9},{9,17},{17,25},{25,1},{2,10},{10... | collective-permute-start | bytes 6291464 | tf_op jit(solution)/shard_map/ppermute | solution.py:21
  115.1 52.3 %copy-start.9 = (bf16[512,2048]{1,0:T(8,128)(2,1)S(1)}, bf16[512,2048]{1,0:T(8,128)(2,1)}, u32[]{:S(2)}) copy-start(bf16[512,2048]{1,0:T(8,128)(2,1)} %copy-done.8) | copy-start | bytes 6291460
  408.0 58.1 %all-gather.8.cloned.1.call-start = ((), (), s32[]{:S(2)}) async-start(), calls=%async_computation.2 | async-start | bytes 2359296 | tf_op jit(solution)/shard_map/all_gather | solution.py:163
  480.6 7.3 %copy-start.3 = (f32[2,4096,512]{1,2,0:T(8,128)}, f32[2,4096,512]{1,2,0:T(8,128)S(1)}, u32[]{:S(2)}) copy-start(f32[2,4096,512]{1,2,0:T(8,128)S(1)} %get-tuple-element.470) | copy-start | bytes 50331652 | tf_op jit(solution)/shard_map/while/body/eval_jaxpr/cond
  482.5 5.3 copy-start.6
  510.3 4.3 copy-start
  516.0 4.4 copy-start.1
  516.0 5.3 copy-start.4
  535.8 4.3 copy-start
  541.5 4.4 copy-start.1
  541.5 5.3 copy-start.4
  561.3 4.3 copy-start
  567.0 4.4 copy-start.1
  567.0 5.3 copy-start.4
  586.8 4.3 copy-start
  592.5 4.4 copy-start.1
  592.5 5.3 copy-start.4
  612.3 4.3 copy-start
  618.0 4.4 copy-start.1
  618.0 5.3 copy-start.4
  643.5 4.4 copy-start.1
  643.5 5.3 copy-start.4
  663.3 4.3 copy-start
  669.0 4.4 copy-start.1
  669.0 5.3 copy-start.4
  (13 other events, 29.3 us)
Sparse Core Ops, SparseCore 0:
  13.6 361.5 all-gather.3
  408.1 27.7 all-gather.5
  437.5 28.5 all-gather.7
